TPU v7x, 32 devices: a whole 2x2x4 slice. The times are simulated.
32 devices in a mesh: layer: 8 (over z, x), split: 4 (over y, core).
Axes of the slice: x: 2, y: 2, z: 4, core: 2. Of those that a mesh axis runs over, the one named last changes fastest.
Arguments:
- right_side: float32 [32, 512, 128], P('layer', 'split'), may hold values from -6 to 6
- diagonal: float32 [32, 512, 128], P('layer', 'split'), may hold values from 0.1 to 1
- inverses: float32 [32, 512, 512], P('layer', None, 'split'), may hold values from -1 to 1, as said below
Outputs:
- solution_field: float32 [32, 512, 128], P('layer', 'split')
- residual: float32 [32, 512, 128], P('layer', 'split')
Inputs may be any that keep to these rules, and one draw needn't show every extreme that they name: `inverses`: each plane's inverse is a diagonal matrix with entries between 0.5 and 1 plus a dense coupling with zero diagonal and spectral norm below 0.2.
All inputs are finite; a program needn't handle non-finite values.
Results may differ from a plain program's by a relative error of at most 0.0003.
Values sent between devices are 32-bit elements; how exact they have to be, the bound alone decides.
No kernel may reach another device: no remote copies, remote signals or barrier semaphores. Data moves between devices by JAX's collectives and lax.ppermute only.
A program may use at most 64 MiB of HBM per device.

v0:
```python
import jax
import jax.numpy as jnp
from jax import lax
from jax.sharding import PartitionSpec as P


def with_halo(x, sides, width):
    for axis, dim in sides:
        size, length = (lax.axis_size(axis), x.shape[dim])
        up = [(i, (i + 1) % size) for i in range(size - 1)]
        down = [(j, i) for i, j in up]
        last = lax.slice_in_dim(x, length - width, length, axis=dim)
        first = lax.slice_in_dim(x, 0, width, axis=dim)
        before = lax.ppermute(last, axis, up)
        after = lax.ppermute(first, axis, down)
        x = jnp.concatenate([before, x, after], axis=dim)
    return x


def from_behind(block, axis, distance):
    devices = range(lax.axis_size(axis))
    route = [(i - distance, i) for i in devices if i - distance in devices]
    return lax.ppermute(block, axis, route)


def stencil(values, diagonal):
    padded = with_halo(values, (("layer", 0), ("split", 1)), 1)
    beside = padded[2:, 1:-1, :] + padded[:-2, 1:-1, :]
    beside = beside + padded[1:-1, 2:, :] + padded[1:-1, :-2, :]
    centre_part = padded[1:-1, 1:-1, :]
    y_upper = jnp.pad(centre_part[:, :, 1:], ((0, 0), (0, 0), (0, 1)))
    y_lower = jnp.pad(centre_part[:, :, :-1], ((0, 0), (0, 0), (1, 0)))
    return (6.0 + diagonal) * values - beside - y_upper - y_lower


def down_local(matrices, portion, carried):

    def down_advance(state, inputs):
        matrix, source = inputs
        state = jnp.dot(matrix, source + state, precision=lax.Precision.HIGHEST)
        return (state, state)

    return lax.scan(down_advance, carried, (matrices, portion))


def up_local(matrices, portion, carried):

    def up_advance(state, inputs):
        matrix, below = inputs
        state = below + jnp.dot(matrix, state, precision=lax.Precision.HIGHEST)
        return (state, state)

    return lax.scan(up_advance, carried, (matrices, portion), reverse=True)


def chain_sweep(sweep_fn, matrices, source, sender, anchor, nblocks):
    depth_count = lax.axis_size("layer")
    block_width = source.shape[2] // nblocks
    plane_shape = (source.shape[1], block_width)
    result = jnp.zeros_like(source)
    incoming = jnp.zeros(plane_shape, jnp.float32)

    def chain_advance(turn, state):
        result, incoming = state
        block_raw = turn - anchor
        active = jnp.logical_and(block_raw >= 0, block_raw < nblocks)

        def working(unused):
            return sweep_fn(matrices, source, incoming)

        def resting(unused):
            return (jnp.zeros(plane_shape, jnp.float32), jnp.zeros_like(source))

        outgoing, stacked = lax.cond(active, working, resting, None)
        previous = result
        result = jnp.where(active, stacked, previous)
        return (result, sender(outgoing))

    result, incoming = lax.fori_loop(
        0, depth_count + nblocks - 1, chain_advance, (result, incoming)
    )
    return result


def per_device(right_side, diagonal, inverses):
    matrices = lax.all_gather(inverses, "split", axis=2, tiled=True)
    columns = lax.all_to_all(right_side, "split", split_axis=2, concat_axis=1, tiled=True)
    nblocks = 1
    own_index = lax.axis_index("layer")
    depth_count = lax.axis_size("layer")
    applied_rhs = stencil(right_side, diagonal)

    def send_down(values):
        return from_behind(values, "layer", 1)

    def send_up(values):
        return from_behind(values, "layer", -1)

    lower_sweep = chain_sweep(down_local, matrices, columns, send_down, own_index, nblocks)
    upper_sweep = chain_sweep(
        up_local, matrices, lower_sweep, send_up, depth_count - 1 - own_index, nblocks
    )
    direction = lax.all_to_all(upper_sweep, "split", split_axis=1, concat_axis=2, tiled=True)
    image = stencil(direction, diagonal)
    applied_image = stencil(image, diagonal)
    sums_all = lax.psum(
        (
            jnp.sum(right_side * right_side),
            jnp.sum(right_side * image),
            jnp.sum(applied_rhs * right_side),
            jnp.sum(applied_rhs * image),
            jnp.sum(applied_image * right_side),
            jnp.sum(applied_image * image),
            jnp.sum(applied_rhs * applied_rhs),
            jnp.sum(applied_rhs * applied_image),
            jnp.sum(applied_image * applied_image),
        ),
        ("layer", "split"),
    )
    (
        norm_sq,
        curv_sum,
        rhs_rhs,
        rhs_image,
        image_rhs,
        image_image,
        arhs_arhs,
        arhs_aimage,
        aimage_aimage,
    ) = sums_all
    step_alpha = norm_sq / curv_sum
    middle = right_side - step_alpha * image
    tangent = applied_rhs - step_alpha * applied_image
    cross_sum = (
        rhs_rhs - step_alpha * (rhs_image + image_rhs) + step_alpha * step_alpha * image_image
    )
    self_sum = arhs_arhs - 2.0 * step_alpha * arhs_aimage + step_alpha * step_alpha * aimage_aimage
    step_omega = cross_sum / self_sum
    solution_field = step_alpha * direction + step_omega * middle
    residual = middle - step_omega * tangent
    return (solution_field, residual)


def solution(mesh):
    placed = (P("layer", "split", None), P("layer", "split", None), P("layer", None, "split"))
    return jax.shard_map(
        per_device,
        mesh=mesh,
        in_specs=placed,
        out_specs=(P("layer", "split", None), P("layer", "split", None)),
        check_vma=False,
    )
```

profile of v0, /device:TPU:12, one launch (start us, length us, event | category | flops | bytes accessed | tf_op | source)
XLA Modules:
  0.0 438.9 jit_solution(2182941142321325081)
XLA Ops:
  23.4 21.4 %all-gather.2.cloned.1.call-done = f32[4,512,512]{2,1,0:T(8,128)} async-done(((f32[4,512,128]{2,1,0:T(8,128)}), f32[4,512,512]{2,1,0:T(8,128)}) %all-gather.2.cloned.1.call-update) | async-done | bytes 4194320 | tf_op jit(solution)/shard_map/all_gather | solution.py:86
  44.8 112.2 %while.60 = (s32[]{:T(128)}, f32[4,512,32]{1,2,0:T(8,128)S(1)}, f32[512,32]{0,1:T(8,128)S(1)}, s32[]{:T(128)}, f32[4,512,512]{2,1,0:T(8,128)}, /*index=5*/f32[4,512,32]{1,2,0:T(8,128)S(1)}, s32[]{:T(128)}, s32[]{:T(128)}) while((s32[]{:T(128)}, f32[4,512,32]{1,2,0:T(8,128)S(1)}, f32[512,32]{0,1:T(8,128)S(1)}, s32[]{:T(128)}, ...), condition=%wide.region_7.8_spmd.clone, body=%wide.region_2.7_spmd.clone.sunk | while | flops 100810760 | bytes 2623315 | solution.py:79
  55.9 22.0 %collective-permute-done.1 = f32[512,32]{0,1:T(8,128)S(1)} collective-permute-done((f32[512,32]{0,1:T(8,128)S(1)}, f32[512,32]{0,1:T(8,128)S(1)}, u32[]{:S(2)}, u32[]{:S(2)}) %collective-permute-start.1) | collective-permute-done | bytes 65568 | tf_op jit(solution)/shard_map/while/body/eval_jaxpr/ppermute | solution.py:23
  77.9 11.7 %conditional.6 = (f32[512,32]{0,1:T(8,128)S(1)}, f32[4,512,32]{1,2,0:T(8,128)}) conditional(s32[]{:T(128)} %convert_element_type.26, () %tuple.150, (f32[4,512,512]{2,1,0:T(8,128)}, f32[4,512,32]{1,2,0:T(8,128)S(1)}, f32[512,32]{0,1:T(8,128)S(1)}) %tuple.151), branch_computations={%region_3.3_spmd, %region_4.6_spmd} | conditional | flops 100679680 | bytes 1574541 | solution.py:74
  77.9 11.7 %while.58 = (s32[]{:T(128)}, f32[512,32]{0,1:T(8,128)S(1)}, f32[4,512,32]{1,2,0:T(8,128)}, f32[4,512,512]{2,1,0:T(8,128)}, f32[4,512,32]{1,2,0:T(8,128)S(1)}, /*index=5*/s32[]{:T(128)}) while((s32[]{:T(128)}, f32[512,32]{0,1:T(8,128)S(1)}, f32[4,512,32]{1,2,0:T(8,128)}, f32[4,512,512]{2,1,0:T(8,128)}, f32[4,512,32]{1,2,0:T(8,128)S(1)}, ...), condition=%wide.region_6.5_spmd, body=%wide.region_5.4_spmd.sunk | while | flops 100679680 | bytes 1443397 | solution.py:43
  97.4 12.0 %collective-permute-start.1 = (f32[512,32]{0,1:T(8,128)S(1)}, f32[512,32]{0,1:T(8,128)S(1)}, u32[]{:S(2)}, u32[]{:S(2)}) collective-permute-start(f32[512,32]{0,1:T(8,128)S(1)} %get-tuple-element.643), channel_id=1, source_target_pairs={{0,4},{4,8},{8,12},{12,16},{16,20},{20,24},{24,28},{1,5},{5,9},{9,... | collective-permute-start | bytes 196616 | tf_op jit(solution)/shard_map/while/body/eval_jaxpr/ppermute | solution.py:23
  119.8 12.9 %collective-permute-start.1 = (f32[512,32]{0,1:T(8,128)S(1)}, f32[512,32]{0,1:T(8,128)S(1)}, u32[]{:S(2)}, u32[]{:S(2)}) collective-permute-start(f32[512,32]{0,1:T(8,128)S(1)} %get-tuple-element.643), channel_id=1, source_target_pairs={{0,4},{4,8},{8,12},{12,16},{16,20},{20,24},{24,28},{1,5},{5,9},{9,... | collective-permute-start | bytes 196616 | tf_op jit(solution)/shard_map/while/body/eval_jaxpr/ppermute | solution.py:23
  135.3 5.2 %collective-permute-start.1 = (f32[512,32]{0,1:T(8,128)S(1)}, f32[512,32]{0,1:T(8,128)S(1)}, u32[]{:S(2)}, u32[]{:S(2)}) collective-permute-start(f32[512,32]{0,1:T(8,128)S(1)} %get-tuple-element.643), channel_id=1, source_target_pairs={{0,4},{4,8},{8,12},{12,16},{16,20},{20,24},{24,28},{1,5},{5,9},{9,... | collective-permute-start | bytes 196616 | tf_op jit(solution)/shard_map/while/body/eval_jaxpr/ppermute | solution.py:23
  143.1 12.0 %collective-permute-start.1 = (f32[512,32]{0,1:T(8,128)S(1)}, f32[512,32]{0,1:T(8,128)S(1)}, u32[]{:S(2)}, u32[]{:S(2)}) collective-permute-start(f32[512,32]{0,1:T(8,128)S(1)} %get-tuple-element.643), channel_id=1, source_target_pairs={{0,4},{4,8},{8,12},{12,16},{16,20},{20,24},{24,28},{1,5},{5,9},{9,... | collective-permute-start | bytes 196616 | tf_op jit(solution)/shard_map/while/body/eval_jaxpr/ppermute | solution.py:23
  157.0 155.7 %while.61 = (s32[]{:T(128)}, f32[4,512,32]{1,2,0:T(8,128)S(1)}, f32[512,32]{0,1:T(8,128)S(1)}, s32[]{:T(128)}, f32[4,512,32]{1,2,0:T(8,128)S(1)}, /*index=5*/f32[4,512,512]{2,1,0:T(8,128)}, s32[]{:T(128)}, s32[]{:T(128)}) while((s32[]{:T(128)}, f32[4,512,32]{1,2,0:T(8,128)S(1)}, f32[512,32]{0,1:T(8,128)S(1)}, s32[]{:T(128)}, ...), condition=%wide.region_13.14_spmd.clone, body=%wide.region_8.13_spmd.clone.sunk | while | flops 100810760 | bytes 2884979 | solution.py:79
  159.8 5.4 %collective-permute-done = f32[512,32]{0,1:T(8,128)S(1)} collective-permute-done((f32[512,32]{0,1:T(8,128)S(1)}, f32[512,32]{0,1:T(8,128)S(1)}, u32[]{:S(2)}, u32[]{:S(2)}) %collective-permute-start) | collective-permute-done | bytes 65568 | tf_op jit(solution)/shard_map/while/body/eval_jaxpr/ppermute | solution.py:23
  168.2 13.4 %collective-permute-done = f32[512,32]{0,1:T(8,128)S(1)} collective-permute-done((f32[512,32]{0,1:T(8,128)S(1)}, f32[512,32]{0,1:T(8,128)S(1)}, u32[]{:S(2)}, u32[]{:S(2)}) %collective-permute-start) | collective-permute-done | bytes 65568 | tf_op jit(solution)/shard_map/while/body/eval_jaxpr/ppermute | solution.py:23
  184.4 5.0 %collective-permute-done = f32[512,32]{0,1:T(8,128)S(1)} collective-permute-done((f32[512,32]{0,1:T(8,128)S(1)}, f32[512,32]{0,1:T(8,128)S(1)}, u32[]{:S(2)}, u32[]{:S(2)}) %collective-permute-start) | collective-permute-done | bytes 65568 | tf_op jit(solution)/shard_map/while/body/eval_jaxpr/ppermute | solution.py:23
  192.2 11.9 %collective-permute-done = f32[512,32]{0,1:T(8,128)S(1)} collective-permute-done((f32[512,32]{0,1:T(8,128)S(1)}, f32[512,32]{0,1:T(8,128)S(1)}, u32[]{:S(2)}, u32[]{:S(2)}) %collective-permute-start) | collective-permute-done | bytes 65568 | tf_op jit(solution)/shard_map/while/body/eval_jaxpr/ppermute | solution.py:23
  206.9 62.3 %collective-permute-done = f32[512,32]{0,1:T(8,128)S(1)} collective-permute-done((f32[512,32]{0,1:T(8,128)S(1)}, f32[512,32]{0,1:T(8,128)S(1)}, u32[]{:S(2)}, u32[]{:S(2)}) %collective-permute-start) | collective-permute-done | bytes 65568 | tf_op jit(solution)/shard_map/while/body/eval_jaxpr/ppermute | solution.py:23
  269.2 12.4 %conditional.7 = (f32[512,32]{0,1:T(8,128)S(1)}, f32[4,512,32]{1,2,0:T(8,128)}) conditional(s32[]{:T(128)} %convert_element_type.27, () %tuple.153, (f32[4,512,32]{1,2,0:T(8,128)S(1)}, f32[4,512,512]{2,1,0:T(8,128)}, f32[512,32]{0,1:T(8,128)S(1)}) %tuple.154), branch_computations={%region_9.9_spmd, %region_10.12_spmd} | conditional | flops 100679680 | bytes 1836205 | solution.py:74
  270.0 11.7 %while.59 = (s32[]{:T(128)}, f32[512,32]{0,1:T(8,128)S(1)}, f32[4,512,32]{1,2,0:T(8,128)}, f32[4,512,32]{1,2,0:T(8,128)S(1)}, f32[4,512,512]{2,1,0:T(8,128)}, /*index=5*/s32[]{:T(128)}, s32[]{:T(128)}) while((s32[]{:T(128)}, f32[512,32]{0,1:T(8,128)S(1)}, f32[4,512,32]{1,2,0:T(8,128)}, f32[4,512,32]{1,2,0:T(8,128)S(1)}, ...), condition=%wide.region_12.11_spmd, body=%wide.region_11.10_spmd.sunk | while | flops 100679680 | bytes 1442905 | solution.py:53
  288.5 14.5 %collective-permute-start = (f32[512,32]{0,1:T(8,128)S(1)}, f32[512,32]{0,1:T(8,128)S(1)}, u32[]{:S(2)}, u32[]{:S(2)}) collective-permute-start(f32[512,32]{0,1:T(8,128)S(1)} %get-tuple-element.651), channel_id=1, source_target_pairs={{4,0},{8,4},{12,8},{16,12},{20,16},{24,20},{28,24},{5,1},{9,5},{13... | collective-permute-start | bytes 196616 | tf_op jit(solution)/shard_map/while/body/eval_jaxpr/ppermute | solution.py:23
  305.7 5.2 %collective-permute-start = (f32[512,32]{0,1:T(8,128)S(1)}, f32[512,32]{0,1:T(8,128)S(1)}, u32[]{:S(2)}, u32[]{:S(2)}) collective-permute-start(f32[512,32]{0,1:T(8,128)S(1)} %get-tuple-element.651), channel_id=1, source_target_pairs={{4,0},{8,4},{12,8},{16,12},{20,16},{24,20},{28,24},{5,1},{9,5},{13... | collective-permute-start | bytes 196616 | tf_op jit(solution)/shard_map/while/body/eval_jaxpr/ppermute | solution.py:23
  314.5 5.1 %all-to-all-start.1 = ((f32[4,1,16384]{2,1,0:T(1,128)}), f32[4,1,16384]{2,1,0:T(1,128)S(1)}, u32[]{:S(2)}, u32[]{:S(2)}) async-start(f32[4,1,16384]{2,1,0:T(1,128)} %reshape.6), calls=%async_computation.1 | async-start | bytes 524288 | tf_op jit(solution)/shard_map/all_to_all | solution.py:103
  319.6 4.3 all-to-all-done.1
  326.8 12.7 %collective-permute-start.2 = (f32[1,128,128]{1,2,0:T(8,128)S(1)}, f32[1,128,128]{1,2,0:T(8,128)S(1)}, u32[]{:S(2)}, u32[]{:S(2)}) collective-permute-start(f32[1,128,128]{1,2,0:T(8,128)S(1)} %bitcast.60), channel_id=1, source_target_pairs={{4,0},{8,4},{12,8},{16,12},{20,16},{24,20},{28,24},{5,1},{9,5},{13... | collective-permute-start | bytes 196616 | tf_op jit(solution)/shard_map/ppermute | solution.py:15
  341.8 4.7 %collective-permute-done.3 = f32[1,128,128]{1,2,0:T(8,128)S(1)} collective-permute-done((f32[1,128,128]{1,2,0:T(8,128)S(1)}, f32[1,128,128]{1,2,0:T(8,128)S(1)}, u32[]{:S(2)}, u32[]{:S(2)}) %collective-permute-start.3) | collective-permute-done | bytes 65568 | tf_op jit(solution)/shard_map/ppermute | solution.py:14
  383.4 41.7 %all-reduce.6 = (f32[]{:T(128)}, f32[]{:T(128)}, f32[]{:T(128)}, f32[]{:T(128)}, f32[]{:T(128)}, /*index=5*/f32[]{:T(128)}, f32[]{:T(128)}, f32[]{:T(128)}) all-reduce(f32[]{:T(128)} %get-tuple-element.434, f32[]{:T(128)} %multiply_reduce_fusion.8, f32[]{:T(128)} %get-tuple-element.433, ...), channel_id=1, replica_groups=mesh['layer'=8,'split'=4] {'layer','split'}, use_global_device_ids=true, to_apply=%region_17.18 | all-reduce | flops 8 | bytes 64 | tf_op jit(solution)/shard_map/psum | solution.py:106
  (160 shorter events, 156.3 us)
Async XLA Ops:
  7.2 37.6 %all-gather.2.cloned.1.call-start = ((), (), s32[]{:S(2)}) async-start(), calls=%async_computation.2 | async-start | bytes 5242880 | tf_op jit(solution)/shard_map/all_gather | solution.py:86
  9.7 13.7 %all-to-all-start = ((f32[4,128,128]{1,0,2:T(4,128)}), f32[4,128,128]{1,0,2:T(4,128)S(1)}, u32[]{:S(2)}, u32[]{:S(2)}) async-start(f32[4,128,128]{1,0,2:T(4,128)} %copy.44), calls=%async_computation | async-start | bytes 524288 | tf_op jit(solution)/shard_map/all_to_all | solution.py:87
  14.7 326.8 %collective-permute-start.6 = (f32[1,128,128]{1,2,0:T(8,128)S(1)}, f32[1,128,128]{1,2,0:T(8,128)S(1)}, u32[]{:S(2)}, u32[]{:S(2)}) collective-permute-start(f32[1,128,128]{1,2,0:T(8,128)S(1)} %get-tuple-element.507), channel_id=1, source_target_pairs={{4,0},{8,4},{12,8},{16,12},{20,16},{24,20},{28,24},{5,1},{9,5},{13... | collective-permute-start | bytes 196616 | tf_op jit(solution)/shard_map/ppermute | solution.py:15
  18.0 323.5 %collective-permute-start.7 = (f32[1,128,128]{1,2,0:T(8,128)S(1)}, f32[1,128,128]{1,2,0:T(8,128)S(1)}, u32[]{:S(2)}, u32[]{:S(2)}) collective-permute-start(f32[1,128,128]{1,2,0:T(8,128)S(1)} %get-tuple-element.506), channel_id=1, source_target_pairs={{0,4},{4,8},{8,12},{12,16},{16,20},{20,24},{24,28},{1,5},{5,9},{9,... | collective-permute-start | bytes 196616 | tf_op jit(solution)/shard_map/ppermute | solution.py:14
  53.3 24.6 %collective-permute-start.1 = (f32[512,32]{0,1:T(8,128)S(1)}, f32[512,32]{0,1:T(8,128)S(1)}, u32[]{:S(2)}, u32[]{:S(2)}) collective-permute-start(f32[512,32]{0,1:T(8,128)S(1)} %get-tuple-element.643), channel_id=1, source_target_pairs={{0,4},{4,8},{8,12},{12,16},{16,20},{20,24},{24,28},{1,5},{5,9},{9,... | collective-permute-start | bytes 196616 | tf_op jit(solution)/shard_map/while/body/eval_jaxpr/ppermute | solution.py:23
  89.6 7.1 %collective-permute-start.1 = (f32[512,32]{0,1:T(8,128)S(1)}, f32[512,32]{0,1:T(8,128)S(1)}, u32[]{:S(2)}, u32[]{:S(2)}) collective-permute-start(f32[512,32]{0,1:T(8,128)S(1)} %get-tuple-element.643), channel_id=1, source_target_pairs={{0,4},{4,8},{8,12},{12,16},{16,20},{20,24},{24,28},{1,5},{5,9},{9,... | collective-permute-start | bytes 196616 | tf_op jit(solution)/shard_map/while/body/eval_jaxpr/ppermute | solution.py:23
  97.4 13.9 %collective-permute-start.1 = (f32[512,32]{0,1:T(8,128)S(1)}, f32[512,32]{0,1:T(8,128)S(1)}, u32[]{:S(2)}, u32[]{:S(2)}) collective-permute-start(f32[512,32]{0,1:T(8,128)S(1)} %get-tuple-element.643), channel_id=1, source_target_pairs={{0,4},{4,8},{8,12},{12,16},{16,20},{20,24},{24,28},{1,5},{5,9},{9,... | collective-permute-start | bytes 196616 | tf_op jit(solution)/shard_map/while/body/eval_jaxpr/ppermute | solution.py:23
  119.8 14.8 %collective-permute-start.1 = (f32[512,32]{0,1:T(8,128)S(1)}, f32[512,32]{0,1:T(8,128)S(1)}, u32[]{:S(2)}, u32[]{:S(2)}) collective-permute-start(f32[512,32]{0,1:T(8,128)S(1)} %get-tuple-element.643), channel_id=1, source_target_pairs={{0,4},{4,8},{8,12},{12,16},{16,20},{20,24},{24,28},{1,5},{5,9},{9,... | collective-permute-start | bytes 196616 | tf_op jit(solution)/shard_map/while/body/eval_jaxpr/ppermute | solution.py:23
  143.1 13.9 %collective-permute-start.1 = (f32[512,32]{0,1:T(8,128)S(1)}, f32[512,32]{0,1:T(8,128)S(1)}, u32[]{:S(2)}, u32[]{:S(2)}) collective-permute-start(f32[512,32]{0,1:T(8,128)S(1)} %get-tuple-element.643), channel_id=1, source_target_pairs={{0,4},{4,8},{8,12},{12,16},{16,20},{20,24},{24,28},{1,5},{5,9},{9,... | collective-permute-start | bytes 196616 | tf_op jit(solution)/shard_map/while/body/eval_jaxpr/ppermute | solution.py:23
  157.7 7.4 %collective-permute-start = (f32[512,32]{0,1:T(8,128)S(1)}, f32[512,32]{0,1:T(8,128)S(1)}, u32[]{:S(2)}, u32[]{:S(2)}) collective-permute-start(f32[512,32]{0,1:T(8,128)S(1)} %get-tuple-element.651), channel_id=1, source_target_pairs={{4,0},{8,4},{12,8},{16,12},{20,16},{24,20},{28,24},{5,1},{9,5},{13... | collective-permute-start | bytes 196616 | tf_op jit(solution)/shard_map/while/body/eval_jaxpr/ppermute | solution.py:23
  165.9 15.7 %collective-permute-start = (f32[512,32]{0,1:T(8,128)S(1)}, f32[512,32]{0,1:T(8,128)S(1)}, u32[]{:S(2)}, u32[]{:S(2)}) collective-permute-start(f32[512,32]{0,1:T(8,128)S(1)} %get-tuple-element.651), channel_id=1, source_target_pairs={{4,0},{8,4},{12,8},{16,12},{20,16},{24,20},{28,24},{5,1},{9,5},{13... | collective-permute-start | bytes 196616 | tf_op jit(solution)/shard_map/while/body/eval_jaxpr/ppermute | solution.py:23
  190.1 14.0 %collective-permute-start = (f32[512,32]{0,1:T(8,128)S(1)}, f32[512,32]{0,1:T(8,128)S(1)}, u32[]{:S(2)}, u32[]{:S(2)}) collective-permute-start(f32[512,32]{0,1:T(8,128)S(1)} %get-tuple-element.651), channel_id=1, source_target_pairs={{4,0},{8,4},{12,8},{16,12},{20,16},{24,20},{28,24},{5,1},{9,5},{13... | collective-permute-start | bytes 196616 | tf_op jit(solution)/shard_map/while/body/eval_jaxpr/ppermute | solution.py:23
  204.8 64.4 %collective-permute-start = (f32[512,32]{0,1:T(8,128)S(1)}, f32[512,32]{0,1:T(8,128)S(1)}, u32[]{:S(2)}, u32[]{:S(2)}) collective-permute-start(f32[512,32]{0,1:T(8,128)S(1)} %get-tuple-element.651), channel_id=1, source_target_pairs={{4,0},{8,4},{12,8},{16,12},{20,16},{24,20},{28,24},{5,1},{9,5},{13... | collective-permute-start | bytes 196616 | tf_op jit(solution)/shard_map/while/body/eval_jaxpr/ppermute | solution.py:23
  288.5 16.4 %collective-permute-start = (f32[512,32]{0,1:T(8,128)S(1)}, f32[512,32]{0,1:T(8,128)S(1)}, u32[]{:S(2)}, u32[]{:S(2)}) collective-permute-start(f32[512,32]{0,1:T(8,128)S(1)} %get-tuple-element.651), channel_id=1, source_target_pairs={{4,0},{8,4},{12,8},{16,12},{20,16},{24,20},{28,24},{5,1},{9,5},{13... | collective-permute-start | bytes 196616 | tf_op jit(solution)/shard_map/while/body/eval_jaxpr/ppermute | solution.py:23
  314.5 9.4 %all-to-all-start.1 = ((f32[4,1,16384]{2,1,0:T(1,128)}), f32[4,1,16384]{2,1,0:T(1,128)S(1)}, u32[]{:S(2)}, u32[]{:S(2)}) async-start(f32[4,1,16384]{2,1,0:T(1,128)} %reshape.6), calls=%async_computation.1 | async-start | bytes 524288 | tf_op jit(solution)/shard_map/all_to_all | solution.py:103
  326.8 15.1 %collective-permute-start.2 = (f32[1,128,128]{1,2,0:T(8,128)S(1)}, f32[1,128,128]{1,2,0:T(8,128)S(1)}, u32[]{:S(2)}, u32[]{:S(2)}) collective-permute-start(f32[1,128,128]{1,2,0:T(8,128)S(1)} %bitcast.60), channel_id=1, source_target_pairs={{4,0},{8,4},{12,8},{16,12},{20,16},{24,20},{28,24},{5,1},{9,5},{13... | collective-permute-start | bytes 196616 | tf_op jit(solution)/shard_map/ppermute | solution.py:15
  339.5 7.1 %collective-permute-start.3 = (f32[1,128,128]{1,2,0:T(8,128)S(1)}, f32[1,128,128]{1,2,0:T(8,128)S(1)}, u32[]{:S(2)}, u32[]{:S(2)}) collective-permute-start(f32[1,128,128]{1,2,0:T(8,128)S(1)} %bitcast.61), channel_id=1, source_target_pairs={{0,4},{4,8},{8,12},{12,16},{16,20},{20,24},{24,28},{1,5},{5,9},{9,... | collective-permute-start | bytes 196616 | tf_op jit(solution)/shard_map/ppermute | solution.py:14
  346.8 7.2 %collective-permute-start.4 = (f32[6,1,128]{1,2,0:T(8,128)S(1)}, f32[6,1,128]{1,2,0:T(8,128)S(1)}, u32[]{:S(2)}, u32[]{:S(2)}) collective-permute-start(f32[6,1,128]{1,2,0:T(8,128)S(1)} %get-tuple-element.500), channel_id=1, source_target_pairs={{1,0},{2,1},{3,2},{5,4},{6,5},{7,6},{9,8},{10,9},{11,10},{13,12},{... | collective-permute-start | bytes 9224 | tf_op jit(solution)/shard_map/ppermute | solution.py:15
  348.7 9.1 %collective-permute-start.5 = (f32[6,1,128]{1,2,0:T(8,128)S(1)}, f32[6,1,128]{1,2,0:T(8,128)S(1)}, u32[]{:S(2)}, u32[]{:S(2)}) collective-permute-start(f32[6,1,128]{1,2,0:T(8,128)S(1)} %get-tuple-element.501), channel_id=1, source_target_pairs={{0,1},{1,2},{2,3},{4,5},{5,6},{6,7},{8,9},{9,10},{10,11},{12,13},{... | collective-permute-start | bytes 9224 | tf_op jit(solution)/shard_map/ppermute | solution.py:14
  358.1 10.4 %collective-permute-start.10 = (f32[1,128,128]{1,2,0:T(8,128)S(1)}, f32[1,128,128]{1,2,0:T(8,128)S(1)}, u32[]{:S(2)}, u32[]{:S(2)}) collective-permute-start(f32[1,128,128]{1,2,0:T(8,128)S(1)} %get-tuple-element.503), channel_id=1, source_target_pairs={{4,0},{8,4},{12,8},{16,12},{20,16},{24,20},{28,24},{5,1},{9,5},{13... | collective-permute-start | bytes 196616 | tf_op jit(solution)/shard_map/ppermute | solution.py:15
  364.1 9.7 %collective-permute-start.8 = (f32[6,1,128]{1,2,0:T(8,128)S(1)}, f32[6,1,128]{1,2,0:T(8,128)S(1)}, u32[]{:S(2)}, u32[]{:S(2)}) collective-permute-start(f32[6,1,128]{1,2,0:T(8,128)S(1)} %get-tuple-element.498), channel_id=1, source_target_pairs={{1,0},{2,1},{3,2},{5,4},{6,5},{7,6},{9,8},{10,9},{11,10},{13,12},{... | collective-permute-start | bytes 9224 | tf_op jit(solution)/shard_map/ppermute | solution.py:15
  366.1 9.1 %collective-permute-start.9 = (f32[6,1,128]{1,2,0:T(8,128)S(1)}, f32[6,1,128]{1,2,0:T(8,128)S(1)}, u32[]{:S(2)}, u32[]{:S(2)}) collective-permute-start(f32[6,1,128]{1,2,0:T(8,128)S(1)} %get-tuple-element.499), channel_id=1, source_target_pairs={{0,1},{1,2},{2,3},{4,5},{5,6},{6,7},{8,9},{9,10},{10,11},{12,13},{... | collective-permute-start | bytes 9224 | tf_op jit(solution)/shard_map/ppermute | solution.py:14
  368.8 8.4 %collective-permute-start.12 = (f32[6,1,128]{1,2,0:T(8,128)S(1)}, f32[6,1,128]{1,2,0:T(8,128)S(1)}, u32[]{:S(2)}, u32[]{:S(2)}) collective-permute-start(f32[6,1,128]{1,2,0:T(8,128)S(1)} %get-tuple-element.496), channel_id=1, source_target_pairs={{1,0},{2,1},{3,2},{5,4},{6,5},{7,6},{9,8},{10,9},{11,10},{13,12},{... | collective-permute-start | bytes 9224 | tf_op jit(solution)/shard_map/ppermute | solution.py:15
  371.9 9.1 %collective-permute-start.13 = (f32[6,1,128]{1,2,0:T(8,128)S(1)}, f32[6,1,128]{1,2,0:T(8,128)S(1)}, u32[]{:S(2)}, u32[]{:S(2)}) collective-permute-start(f32[6,1,128]{1,2,0:T(8,128)S(1)} %get-tuple-element.497), channel_id=1, source_target_pairs={{0,1},{1,2},{2,3},{4,5},{5,6},{6,7},{8,9},{9,10},{10,11},{12,13},{... | collective-permute-start | bytes 9224 | tf_op jit(solution)/shard_map/ppermute | solution.py:14
  (7 other events, 48.4 us)
Sparse Core Ops, SparseCore 0:
  9.5 35.1 all-gather.1
where the time goes:
time: 441 us; the launch traced here: 439 us
  waiting for transfers between devices  189 us (43%)
  starting transfers between devices  134 us (30%)
  blocking collectives  41.7 us (9%)
  matrix products  23.3 us (5%)
  local copies, waits for them, and re-layouts  20.9 us (5%)
  between operations  20.8 us (5%)
  other arithmetic  8.15 us (2%)
    ppermute x16, waiting for transfers between devices, from_behind(): return lax.ppermute(block, axis, route)  144 us
    ppermute x16, starting transfers between devices, from_behind(): return lax.ppermute(block, axis, route)  85.4 us
    psum x1, blocking collectives, per_device(): lax.psum((jnp.sum(right_side * right_side), jnp.sum(right_side * image),...  41.7 us
    ppermute x6, starting transfers between devices, with_halo(): after = lax.ppermute(first, axis, down)  26.3 us
    all_gather x1, waiting for transfers between devices, per_device(): matrices = lax.all_gather(inverses, 'split', axis=2, tiled=True)  21.4 us
    ppermute x6, starting transfers between devices, with_halo(): before = lax.ppermute(last, axis, up)  13.7 us
    ppermute x6, waiting for transfers between devices, with_halo(): before = lax.ppermute(last, axis, up)  13.7 us
    dot_general x4, matrix products, down_advance(): state = jnp.dot(matrix, source + state, precision=lax.Precision.HIGHEST)  11.7 us
  transfers between devices with their start and end apart: 31, of which 24 were waited for; matrix products, arithmetic and copies ran while one was open for 11% of the time, Pallas kernels for 0%

commit v1 on v0

--- a/solution.py
+++ b/solution.py
@@ -104,18 +104,21 @@
     image = stencil(direction, diagonal)
     applied_image = stencil(image, diagonal)
     sums_all = lax.psum(
-        (
-            jnp.sum(right_side * right_side),
-            jnp.sum(right_side * image),
-            jnp.sum(applied_rhs * right_side),
-            jnp.sum(applied_rhs * image),
-            jnp.sum(applied_image * right_side),
-            jnp.sum(applied_image * image),
-            jnp.sum(applied_rhs * applied_rhs),
-            jnp.sum(applied_rhs * applied_image),
-            jnp.sum(applied_image * applied_image),
+        lax.psum(
+            (
+                jnp.sum(right_side * right_side),
+                jnp.sum(right_side * image),
+                jnp.sum(applied_rhs * right_side),
+                jnp.sum(applied_rhs * image),
+                jnp.sum(applied_image * right_side),
+                jnp.sum(applied_image * image),
+                jnp.sum(applied_rhs * applied_rhs),
+                jnp.sum(applied_rhs * applied_image),
+                jnp.sum(applied_image * applied_image),
+            ),
+            "layer",
         ),
-        ("layer", "split"),
+        "split",
     )
     (
         norm_sq,

time: 441 us -> 426 us (0.966)
  blocking collectives: 41.7 us -> 24 us
    psum x1, blocking collectives: 41.7 us -> 17.5 us  [per_device(): lax.psum((jnp.sum(right_side * right_side), jnp.sum(right_side * image),...]
    psum x0 -> x1, blocking collectives: none -> 6.47 us  [per_device(): lax.psum(lax.psum((jnp.sum(right_side * right_side), jnp.sum(right_side *...]
  transfers between devices with their start and end apart: 31 -> 31, of which waited for: 24 -> 24; matrix products, arithmetic and copies ran while one was open for 11% -> 12% of each run, Pallas kernels for 0% -> 0%
where the time goes in v1:
time: 426 us; the launch traced here: 421 us
  waiting for transfers between devices  189 us (44%)
  starting transfers between devices  134 us (31%)
  blocking collectives  24 us (6%)
  matrix products  23.3 us (5%)
  local copies, waits for them, and re-layouts  20.9 us (5%)
  between operations  20.7 us (5%)
  other arithmetic  8.09 us (2%)
    ppermute x16, waiting for transfers between devices, from_behind(): return lax.ppermute(block, axis, route)  144 us
    ppermute x16, starting transfers between devices, from_behind(): return lax.ppermute(block, axis, route)  85.4 us
    ppermute x6, starting transfers between devices, with_halo(): after = lax.ppermute(first, axis, down)  26.3 us
    all_gather x1, waiting for transfers between devices, per_device(): matrices = lax.all_gather(inverses, 'split', axis=2, tiled=True)  21.4 us
    psum x1, blocking collectives, per_device(): lax.psum((jnp.sum(right_side * right_side), jnp.sum(right_side * image),...  17.5 us
    ppermute x6, starting transfers between devices, with_halo(): before = lax.ppermute(last, axis, up)  13.7 us
    ppermute x6, waiting for transfers between devices, with_halo(): before = lax.ppermute(last, axis, up)  13.7 us
    dot_general x4, matrix products, down_advance(): state = jnp.dot(matrix, source + state, precision=lax.Precision.HIGHEST)  11.7 us
  transfers between devices with their start and end apart: 31, of which 24 were waited for; matrix products, arithmetic and copies ran while one was open for 12% of the time, Pallas kernels for 0%

profile of v1, /device:TPU:12, one launch (start us, length us, event | category | flops | bytes accessed | tf_op | source)
XLA Modules:
  0.0 421.2 jit_solution(10306473538622307949)
XLA Ops:
  23.3 21.4 %all-gather.2.cloned.1.call-done = f32[4,512,512]{2,1,0:T(8,128)} async-done(((f32[4,512,128]{2,1,0:T(8,128)}), f32[4,512,512]{2,1,0:T(8,128)}) %all-gather.2.cloned.1.call-update) | async-done | bytes 4194320 | tf_op jit(solution)/shard_map/all_gather | solution.py:86
  44.8 112.2 %while.60 = (s32[]{:T(128)}, f32[4,512,32]{1,2,0:T(8,128)S(1)}, f32[512,32]{0,1:T(8,128)S(1)}, s32[]{:T(128)}, f32[4,512,512]{2,1,0:T(8,128)}, /*index=5*/f32[4,512,32]{1,2,0:T(8,128)S(1)}, s32[]{:T(128)}, s32[]{:T(128)}) while((s32[]{:T(128)}, f32[4,512,32]{1,2,0:T(8,128)S(1)}, f32[512,32]{0,1:T(8,128)S(1)}, s32[]{:T(128)}, ...), condition=%wide.region_8.9_spmd.clone, body=%wide.region_3.8_spmd.clone.sunk | while | flops 100810760 | bytes 2623315 | solution.py:79
  55.9 22.0 %collective-permute-done.1 = f32[512,32]{0,1:T(8,128)S(1)} collective-permute-done((f32[512,32]{0,1:T(8,128)S(1)}, f32[512,32]{0,1:T(8,128)S(1)}, u32[]{:S(2)}, u32[]{:S(2)}) %collective-permute-start.1) | collective-permute-done | bytes 65568 | tf_op jit(solution)/shard_map/while/body/eval_jaxpr/ppermute | solution.py:23
  77.9 11.7 %conditional.6 = (f32[512,32]{0,1:T(8,128)S(1)}, f32[4,512,32]{1,2,0:T(8,128)}) conditional(s32[]{:T(128)} %convert_element_type.26, () %tuple.150, (f32[4,512,512]{2,1,0:T(8,128)}, f32[4,512,32]{1,2,0:T(8,128)S(1)}, f32[512,32]{0,1:T(8,128)S(1)}) %tuple.151), branch_computations={%region_4.4_spmd, %region_5.7_spmd} | conditional | flops 100679680 | bytes 1574541 | solution.py:74
  77.9 11.7 %while.58 = (s32[]{:T(128)}, f32[512,32]{0,1:T(8,128)S(1)}, f32[4,512,32]{1,2,0:T(8,128)}, f32[4,512,512]{2,1,0:T(8,128)}, f32[4,512,32]{1,2,0:T(8,128)S(1)}, /*index=5*/s32[]{:T(128)}) while((s32[]{:T(128)}, f32[512,32]{0,1:T(8,128)S(1)}, f32[4,512,32]{1,2,0:T(8,128)}, f32[4,512,512]{2,1,0:T(8,128)}, f32[4,512,32]{1,2,0:T(8,128)S(1)}, ...), condition=%wide.region_7.6_spmd, body=%wide.region_6.5_spmd.sunk | while | flops 100679680 | bytes 1443397 | solution.py:43
  97.4 12.0 %collective-permute-start.1 = (f32[512,32]{0,1:T(8,128)S(1)}, f32[512,32]{0,1:T(8,128)S(1)}, u32[]{:S(2)}, u32[]{:S(2)}) collective-permute-start(f32[512,32]{0,1:T(8,128)S(1)} %get-tuple-element.651), channel_id=1, source_target_pairs={{0,4},{4,8},{8,12},{12,16},{16,20},{20,24},{24,28},{1,5},{5,9},{9,... | collective-permute-start | bytes 196616 | tf_op jit(solution)/shard_map/while/body/eval_jaxpr/ppermute | solution.py:23
  119.8 12.9 %collective-permute-start.1 = (f32[512,32]{0,1:T(8,128)S(1)}, f32[512,32]{0,1:T(8,128)S(1)}, u32[]{:S(2)}, u32[]{:S(2)}) collective-permute-start(f32[512,32]{0,1:T(8,128)S(1)} %get-tuple-element.651), channel_id=1, source_target_pairs={{0,4},{4,8},{8,12},{12,16},{16,20},{20,24},{24,28},{1,5},{5,9},{9,... | collective-permute-start | bytes 196616 | tf_op jit(solution)/shard_map/while/body/eval_jaxpr/ppermute | solution.py:23
  135.3 5.2 %collective-permute-start.1 = (f32[512,32]{0,1:T(8,128)S(1)}, f32[512,32]{0,1:T(8,128)S(1)}, u32[]{:S(2)}, u32[]{:S(2)}) collective-permute-start(f32[512,32]{0,1:T(8,128)S(1)} %get-tuple-element.651), channel_id=1, source_target_pairs={{0,4},{4,8},{8,12},{12,16},{16,20},{20,24},{24,28},{1,5},{5,9},{9,... | collective-permute-start | bytes 196616 | tf_op jit(solution)/shard_map/while/body/eval_jaxpr/ppermute | solution.py:23
  143.1 12.0 %collective-permute-start.1 = (f32[512,32]{0,1:T(8,128)S(1)}, f32[512,32]{0,1:T(8,128)S(1)}, u32[]{:S(2)}, u32[]{:S(2)}) collective-permute-start(f32[512,32]{0,1:T(8,128)S(1)} %get-tuple-element.651), channel_id=1, source_target_pairs={{0,4},{4,8},{8,12},{12,16},{16,20},{20,24},{24,28},{1,5},{5,9},{9,... | collective-permute-start | bytes 196616 | tf_op jit(solution)/shard_map/while/body/eval_jaxpr/ppermute | solution.py:23
  157.0 155.7 %while.61 = (s32[]{:T(128)}, f32[4,512,32]{1,2,0:T(8,128)S(1)}, f32[512,32]{0,1:T(8,128)S(1)}, s32[]{:T(128)}, f32[4,512,32]{1,2,0:T(8,128)S(1)}, /*index=5*/f32[4,512,512]{2,1,0:T(8,128)}, s32[]{:T(128)}, s32[]{:T(128)}) while((s32[]{:T(128)}, f32[4,512,32]{1,2,0:T(8,128)S(1)}, f32[512,32]{0,1:T(8,128)S(1)}, s32[]{:T(128)}, ...), condition=%wide.region_14.15_spmd.clone, body=%wide.region_9.0_spmd.clone.sunk | while | flops 100810760 | bytes 2884979 | solution.py:79
  159.8 5.4 %collective-permute-done = f32[512,32]{0,1:T(8,128)S(1)} collective-permute-done((f32[512,32]{0,1:T(8,128)S(1)}, f32[512,32]{0,1:T(8,128)S(1)}, u32[]{:S(2)}, u32[]{:S(2)}) %collective-permute-start) | collective-permute-done | bytes 65568 | tf_op jit(solution)/shard_map/while/body/eval_jaxpr/ppermute | solution.py:23
  168.2 13.4 %collective-permute-done = f32[512,32]{0,1:T(8,128)S(1)} collective-permute-done((f32[512,32]{0,1:T(8,128)S(1)}, f32[512,32]{0,1:T(8,128)S(1)}, u32[]{:S(2)}, u32[]{:S(2)}) %collective-permute-start) | collective-permute-done | bytes 65568 | tf_op jit(solution)/shard_map/while/body/eval_jaxpr/ppermute | solution.py:23
  184.4 5.0 %collective-permute-done = f32[512,32]{0,1:T(8,128)S(1)} collective-permute-done((f32[512,32]{0,1:T(8,128)S(1)}, f32[512,32]{0,1:T(8,128)S(1)}, u32[]{:S(2)}, u32[]{:S(2)}) %collective-permute-start) | collective-permute-done | bytes 65568 | tf_op jit(solution)/shard_map/while/body/eval_jaxpr/ppermute | solution.py:23
  192.2 11.9 %collective-permute-done = f32[512,32]{0,1:T(8,128)S(1)} collective-permute-done((f32[512,32]{0,1:T(8,128)S(1)}, f32[512,32]{0,1:T(8,128)S(1)}, u32[]{:S(2)}, u32[]{:S(2)}) %collective-permute-start) | collective-permute-done | bytes 65568 | tf_op jit(solution)/shard_map/while/body/eval_jaxpr/ppermute | solution.py:23
  206.9 62.3 %collective-permute-done = f32[512,32]{0,1:T(8,128)S(1)} collective-permute-done((f32[512,32]{0,1:T(8,128)S(1)}, f32[512,32]{0,1:T(8,128)S(1)}, u32[]{:S(2)}, u32[]{:S(2)}) %collective-permute-start) | collective-permute-done | bytes 65568 | tf_op jit(solution)/shard_map/while/body/eval_jaxpr/ppermute | solution.py:23
  269.2 12.4 %conditional.7 = (f32[512,32]{0,1:T(8,128)S(1)}, f32[4,512,32]{1,2,0:T(8,128)}) conditional(s32[]{:T(128)} %convert_element_type.27, () %tuple.153, (f32[4,512,32]{1,2,0:T(8,128)S(1)}, f32[4,512,512]{2,1,0:T(8,128)}, f32[512,32]{0,1:T(8,128)S(1)}) %tuple.154), branch_computations={%region_10.10_spmd, %region_11.13_spmd} | conditional | flops 100679680 | bytes 1836205 | solution.py:74
  270.0 11.7 %while.59 = (s32[]{:T(128)}, f32[512,32]{0,1:T(8,128)S(1)}, f32[4,512,32]{1,2,0:T(8,128)}, f32[4,512,32]{1,2,0:T(8,128)S(1)}, f32[4,512,512]{2,1,0:T(8,128)}, /*index=5*/s32[]{:T(128)}, s32[]{:T(128)}) while((s32[]{:T(128)}, f32[512,32]{0,1:T(8,128)S(1)}, f32[4,512,32]{1,2,0:T(8,128)}, f32[4,512,32]{1,2,0:T(8,128)S(1)}, ...), condition=%wide.region_13.12_spmd, body=%wide.region_12.11_spmd.sunk | while | flops 100679680 | bytes 1442905 | solution.py:53
  288.5 14.5 %collective-permute-start = (f32[512,32]{0,1:T(8,128)S(1)}, f32[512,32]{0,1:T(8,128)S(1)}, u32[]{:S(2)}, u32[]{:S(2)}) collective-permute-start(f32[512,32]{0,1:T(8,128)S(1)} %get-tuple-element.659), channel_id=1, source_target_pairs={{4,0},{8,4},{12,8},{16,12},{20,16},{24,20},{28,24},{5,1},{9,5},{13... | collective-permute-start | bytes 196616 | tf_op jit(solution)/shard_map/while/body/eval_jaxpr/ppermute | solution.py:23
  305.7 5.2 %collective-permute-start = (f32[512,32]{0,1:T(8,128)S(1)}, f32[512,32]{0,1:T(8,128)S(1)}, u32[]{:S(2)}, u32[]{:S(2)}) collective-permute-start(f32[512,32]{0,1:T(8,128)S(1)} %get-tuple-element.659), channel_id=1, source_target_pairs={{4,0},{8,4},{12,8},{16,12},{20,16},{24,20},{28,24},{5,1},{9,5},{13... | collective-permute-start | bytes 196616 | tf_op jit(solution)/shard_map/while/body/eval_jaxpr/ppermute | solution.py:23
  314.5 5.1 %all-to-all-start.1 = ((f32[4,1,16384]{2,1,0:T(1,128)}), f32[4,1,16384]{2,1,0:T(1,128)S(1)}, u32[]{:S(2)}, u32[]{:S(2)}) async-start(f32[4,1,16384]{2,1,0:T(1,128)} %reshape.6), calls=%async_computation.1 | async-start | bytes 524288 | tf_op jit(solution)/shard_map/all_to_all | solution.py:103
  326.8 12.7 %collective-permute-start.2 = (f32[1,128,128]{1,2,0:T(8,128)S(1)}, f32[1,128,128]{1,2,0:T(8,128)S(1)}, u32[]{:S(2)}, u32[]{:S(2)}) collective-permute-start(f32[1,128,128]{1,2,0:T(8,128)S(1)} %bitcast.60), channel_id=1, source_target_pairs={{4,0},{8,4},{12,8},{16,12},{20,16},{24,20},{28,24},{5,1},{9,5},{13... | collective-permute-start | bytes 196616 | tf_op jit(solution)/shard_map/ppermute | solution.py:15
  341.8 4.7 %collective-permute-done.3 = f32[1,128,128]{1,2,0:T(8,128)S(1)} collective-permute-done((f32[1,128,128]{1,2,0:T(8,128)S(1)}, f32[1,128,128]{1,2,0:T(8,128)S(1)}, u32[]{:S(2)}, u32[]{:S(2)}) %collective-permute-start.3) | collective-permute-done | bytes 65568 | tf_op jit(solution)/shard_map/ppermute | solution.py:14
  383.5 17.5 %all-reduce.6 = (f32[]{:T(128)}, f32[]{:T(128)}, f32[]{:T(128)}, f32[]{:T(128)}, f32[]{:T(128)}, /*index=5*/f32[]{:T(128)}, f32[]{:T(128)}, f32[]{:T(128)}) all-reduce(f32[]{:T(128)} %get-tuple-element.434, f32[]{:T(128)} %multiply_reduce_fusion.8, f32[]{:T(128)} %get-tuple-element.433, ...), channel_id=1, replica_groups=mesh['layer'=8,'split'=4] {'layer'}, use_global_device_ids=true, to_apply=%region_19.20 | all-reduce | flops 8 | bytes 64 | tf_op jit(solution)/shard_map/psum | solution.py:107
  401.0 6.5 %all-reduce.7 = (f32[]{:T(128)}, f32[]{:T(128)}, f32[]{:T(128)}, f32[]{:T(128)}, f32[]{:T(128)}, /*index=5*/f32[]{:T(128)}, f32[]{:T(128)}, f32[]{:T(128)}) all-reduce(f32[]{:T(128)} %get-tuple-element.480, f32[]{:T(128)} %get-tuple-element.481, f32[]{:T(128)} %get-tuple-element.482, ...), channel_id=1, replica_groups=mesh['layer'=8,'split'=4] {'split'}, use_global_device_ids=true, to_apply=%region_20.21 | all-reduce | flops 8 | bytes 64 | tf_op jit(solution)/shard_map/psum | solution.py:106
  (161 shorter events, 160.6 us)
Async XLA Ops:
  7.2 37.6 %all-gather.2.cloned.1.call-start = ((), (), s32[]{:S(2)}) async-start(), calls=%async_computation.2 | async-start | bytes 5242880 | tf_op jit(solution)/shard_map/all_gather | solution.py:86
  9.7 13.6 %all-to-all-start = ((f32[4,128,128]{1,0,2:T(4,128)}), f32[4,128,128]{1,0,2:T(4,128)S(1)}, u32[]{:S(2)}, u32[]{:S(2)}) async-start(f32[4,128,128]{1,0,2:T(4,128)} %copy.44), calls=%async_computation | async-start | bytes 524288 | tf_op jit(solution)/shard_map/all_to_all | solution.py:87
  14.7 326.8 %collective-permute-start.6 = (f32[1,128,128]{1,2,0:T(8,128)S(1)}, f32[1,128,128]{1,2,0:T(8,128)S(1)}, u32[]{:S(2)}, u32[]{:S(2)}) collective-permute-start(f32[1,128,128]{1,2,0:T(8,128)S(1)} %get-tuple-element.515), channel_id=1, source_target_pairs={{4,0},{8,4},{12,8},{16,12},{20,16},{24,20},{28,24},{5,1},{9,5},{13... | collective-permute-start | bytes 196616 | tf_op jit(solution)/shard_map/ppermute | solution.py:15
  18.0 323.5 %collective-permute-start.7 = (f32[1,128,128]{1,2,0:T(8,128)S(1)}, f32[1,128,128]{1,2,0:T(8,128)S(1)}, u32[]{:S(2)}, u32[]{:S(2)}) collective-permute-start(f32[1,128,128]{1,2,0:T(8,128)S(1)} %get-tuple-element.514), channel_id=1, source_target_pairs={{0,4},{4,8},{8,12},{12,16},{16,20},{20,24},{24,28},{1,5},{5,9},{9,... | collective-permute-start | bytes 196616 | tf_op jit(solution)/shard_map/ppermute | solution.py:14
  53.3 24.6 %collective-permute-start.1 = (f32[512,32]{0,1:T(8,128)S(1)}, f32[512,32]{0,1:T(8,128)S(1)}, u32[]{:S(2)}, u32[]{:S(2)}) collective-permute-start(f32[512,32]{0,1:T(8,128)S(1)} %get-tuple-element.651), channel_id=1, source_target_pairs={{0,4},{4,8},{8,12},{12,16},{16,20},{20,24},{24,28},{1,5},{5,9},{9,... | collective-permute-start | bytes 196616 | tf_op jit(solution)/shard_map/while/body/eval_jaxpr/ppermute | solution.py:23
  89.6 7.1 %collective-permute-start.1 = (f32[512,32]{0,1:T(8,128)S(1)}, f32[512,32]{0,1:T(8,128)S(1)}, u32[]{:S(2)}, u32[]{:S(2)}) collective-permute-start(f32[512,32]{0,1:T(8,128)S(1)} %get-tuple-element.651), channel_id=1, source_target_pairs={{0,4},{4,8},{8,12},{12,16},{16,20},{20,24},{24,28},{1,5},{5,9},{9,... | collective-permute-start | bytes 196616 | tf_op jit(solution)/shard_map/while/body/eval_jaxpr/ppermute | solution.py:23
  97.4 13.9 %collective-permute-start.1 = (f32[512,32]{0,1:T(8,128)S(1)}, f32[512,32]{0,1:T(8,128)S(1)}, u32[]{:S(2)}, u32[]{:S(2)}) collective-permute-start(f32[512,32]{0,1:T(8,128)S(1)} %get-tuple-element.651), channel_id=1, source_target_pairs={{0,4},{4,8},{8,12},{12,16},{16,20},{20,24},{24,28},{1,5},{5,9},{9,... | collective-permute-start | bytes 196616 | tf_op jit(solution)/shard_map/while/body/eval_jaxpr/ppermute | solution.py:23
  119.8 14.8 %collective-permute-start.1 = (f32[512,32]{0,1:T(8,128)S(1)}, f32[512,32]{0,1:T(8,128)S(1)}, u32[]{:S(2)}, u32[]{:S(2)}) collective-permute-start(f32[512,32]{0,1:T(8,128)S(1)} %get-tuple-element.651), channel_id=1, source_target_pairs={{0,4},{4,8},{8,12},{12,16},{16,20},{20,24},{24,28},{1,5},{5,9},{9,... | collective-permute-start | bytes 196616 | tf_op jit(solution)/shard_map/while/body/eval_jaxpr/ppermute | solution.py:23
  143.1 13.9 %collective-permute-start.1 = (f32[512,32]{0,1:T(8,128)S(1)}, f32[512,32]{0,1:T(8,128)S(1)}, u32[]{:S(2)}, u32[]{:S(2)}) collective-permute-start(f32[512,32]{0,1:T(8,128)S(1)} %get-tuple-element.651), channel_id=1, source_target_pairs={{0,4},{4,8},{8,12},{12,16},{16,20},{20,24},{24,28},{1,5},{5,9},{9,... | collective-permute-start | bytes 196616 | tf_op jit(solution)/shard_map/while/body/eval_jaxpr/ppermute | solution.py:23
  157.7 7.4 %collective-permute-start = (f32[512,32]{0,1:T(8,128)S(1)}, f32[512,32]{0,1:T(8,128)S(1)}, u32[]{:S(2)}, u32[]{:S(2)}) collective-permute-start(f32[512,32]{0,1:T(8,128)S(1)} %get-tuple-element.659), channel_id=1, source_target_pairs={{4,0},{8,4},{12,8},{16,12},{20,16},{24,20},{28,24},{5,1},{9,5},{13... | collective-permute-start | bytes 196616 | tf_op jit(solution)/shard_map/while/body/eval_jaxpr/ppermute | solution.py:23
  165.9 15.7 %collective-permute-start = (f32[512,32]{0,1:T(8,128)S(1)}, f32[512,32]{0,1:T(8,128)S(1)}, u32[]{:S(2)}, u32[]{:S(2)}) collective-permute-start(f32[512,32]{0,1:T(8,128)S(1)} %get-tuple-element.659), channel_id=1, source_target_pairs={{4,0},{8,4},{12,8},{16,12},{20,16},{24,20},{28,24},{5,1},{9,5},{13... | collective-permute-start | bytes 196616 | tf_op jit(solution)/shard_map/while/body/eval_jaxpr/ppermute | solution.py:23
  190.1 14.0 %collective-permute-start = (f32[512,32]{0,1:T(8,128)S(1)}, f32[512,32]{0,1:T(8,128)S(1)}, u32[]{:S(2)}, u32[]{:S(2)}) collective-permute-start(f32[512,32]{0,1:T(8,128)S(1)} %get-tuple-element.659), channel_id=1, source_target_pairs={{4,0},{8,4},{12,8},{16,12},{20,16},{24,20},{28,24},{5,1},{9,5},{13... | collective-permute-start | bytes 196616 | tf_op jit(solution)/shard_map/while/body/eval_jaxpr/ppermute | solution.py:23
  204.8 64.4 %collective-permute-start = (f32[512,32]{0,1:T(8,128)S(1)}, f32[512,32]{0,1:T(8,128)S(1)}, u32[]{:S(2)}, u32[]{:S(2)}) collective-permute-start(f32[512,32]{0,1:T(8,128)S(1)} %get-tuple-element.659), channel_id=1, source_target_pairs={{4,0},{8,4},{12,8},{16,12},{20,16},{24,20},{28,24},{5,1},{9,5},{13... | collective-permute-start | bytes 196616 | tf_op jit(solution)/shard_map/while/body/eval_jaxpr/ppermute | solution.py:23
  288.5 16.4 %collective-permute-start = (f32[512,32]{0,1:T(8,128)S(1)}, f32[512,32]{0,1:T(8,128)S(1)}, u32[]{:S(2)}, u32[]{:S(2)}) collective-permute-start(f32[512,32]{0,1:T(8,128)S(1)} %get-tuple-element.659), channel_id=1, source_target_pairs={{4,0},{8,4},{12,8},{16,12},{20,16},{24,20},{28,24},{5,1},{9,5},{13... | collective-permute-start | bytes 196616 | tf_op jit(solution)/shard_map/while/body/eval_jaxpr/ppermute | solution.py:23
  314.5 9.4 %all-to-all-start.1 = ((f32[4,1,16384]{2,1,0:T(1,128)}), f32[4,1,16384]{2,1,0:T(1,128)S(1)}, u32[]{:S(2)}, u32[]{:S(2)}) async-start(f32[4,1,16384]{2,1,0:T(1,128)} %reshape.6), calls=%async_computation.1 | async-start | bytes 524288 | tf_op jit(solution)/shard_map/all_to_all | solution.py:103
  326.8 15.1 %collective-permute-start.2 = (f32[1,128,128]{1,2,0:T(8,128)S(1)}, f32[1,128,128]{1,2,0:T(8,128)S(1)}, u32[]{:S(2)}, u32[]{:S(2)}) collective-permute-start(f32[1,128,128]{1,2,0:T(8,128)S(1)} %bitcast.60), channel_id=1, source_target_pairs={{4,0},{8,4},{12,8},{16,12},{20,16},{24,20},{28,24},{5,1},{9,5},{13... | collective-permute-start | bytes 196616 | tf_op jit(solution)/shard_map/ppermute | solution.py:15
  339.5 7.1 %collective-permute-start.3 = (f32[1,128,128]{1,2,0:T(8,128)S(1)}, f32[1,128,128]{1,2,0:T(8,128)S(1)}, u32[]{:S(2)}, u32[]{:S(2)}) collective-permute-start(f32[1,128,128]{1,2,0:T(8,128)S(1)} %bitcast.61), channel_id=1, source_target_pairs={{0,4},{4,8},{8,12},{12,16},{16,20},{20,24},{24,28},{1,5},{5,9},{9,... | collective-permute-start | bytes 196616 | tf_op jit(solution)/shard_map/ppermute | solution.py:14
  346.8 7.2 %collective-permute-start.4 = (f32[6,1,128]{1,2,0:T(8,128)S(1)}, f32[6,1,128]{1,2,0:T(8,128)S(1)}, u32[]{:S(2)}, u32[]{:S(2)}) collective-permute-start(f32[6,1,128]{1,2,0:T(8,128)S(1)} %get-tuple-element.508), channel_id=1, source_target_pairs={{1,0},{2,1},{3,2},{5,4},{6,5},{7,6},{9,8},{10,9},{11,10},{13,12},{... | collective-permute-start | bytes 9224 | tf_op jit(solution)/shard_map/ppermute | solution.py:15
  348.7 9.1 %collective-permute-start.5 = (f32[6,1,128]{1,2,0:T(8,128)S(1)}, f32[6,1,128]{1,2,0:T(8,128)S(1)}, u32[]{:S(2)}, u32[]{:S(2)}) collective-permute-start(f32[6,1,128]{1,2,0:T(8,128)S(1)} %get-tuple-element.509), channel_id=1, source_target_pairs={{0,1},{1,2},{2,3},{4,5},{5,6},{6,7},{8,9},{9,10},{10,11},{12,13},{... | collective-permute-start | bytes 9224 | tf_op jit(solution)/shard_map/ppermute | solution.py:14
  358.1 10.4 %collective-permute-start.10 = (f32[1,128,128]{1,2,0:T(8,128)S(1)}, f32[1,128,128]{1,2,0:T(8,128)S(1)}, u32[]{:S(2)}, u32[]{:S(2)}) collective-permute-start(f32[1,128,128]{1,2,0:T(8,128)S(1)} %get-tuple-element.511), channel_id=1, source_target_pairs={{4,0},{8,4},{12,8},{16,12},{20,16},{24,20},{28,24},{5,1},{9,5},{13... | collective-permute-start | bytes 196616 | tf_op jit(solution)/shard_map/ppermute | solution.py:15
  364.1 9.7 %collective-permute-start.8 = (f32[6,1,128]{1,2,0:T(8,128)S(1)}, f32[6,1,128]{1,2,0:T(8,128)S(1)}, u32[]{:S(2)}, u32[]{:S(2)}) collective-permute-start(f32[6,1,128]{1,2,0:T(8,128)S(1)} %get-tuple-element.506), channel_id=1, source_target_pairs={{1,0},{2,1},{3,2},{5,4},{6,5},{7,6},{9,8},{10,9},{11,10},{13,12},{... | collective-permute-start | bytes 9224 | tf_op jit(solution)/shard_map/ppermute | solution.py:15
  366.1 9.1 %collective-permute-start.9 = (f32[6,1,128]{1,2,0:T(8,128)S(1)}, f32[6,1,128]{1,2,0:T(8,128)S(1)}, u32[]{:S(2)}, u32[]{:S(2)}) collective-permute-start(f32[6,1,128]{1,2,0:T(8,128)S(1)} %get-tuple-element.507), channel_id=1, source_target_pairs={{0,1},{1,2},{2,3},{4,5},{5,6},{6,7},{8,9},{9,10},{10,11},{12,13},{... | collective-permute-start | bytes 9224 | tf_op jit(solution)/shard_map/ppermute | solution.py:14
  368.8 8.4 %collective-permute-start.12 = (f32[6,1,128]{1,2,0:T(8,128)S(1)}, f32[6,1,128]{1,2,0:T(8,128)S(1)}, u32[]{:S(2)}, u32[]{:S(2)}) collective-permute-start(f32[6,1,128]{1,2,0:T(8,128)S(1)} %get-tuple-element.504), channel_id=1, source_target_pairs={{1,0},{2,1},{3,2},{5,4},{6,5},{7,6},{9,8},{10,9},{11,10},{13,12},{... | collective-permute-start | bytes 9224 | tf_op jit(solution)/shard_map/ppermute | solution.py:15
  371.9 9.1 %collective-permute-start.13 = (f32[6,1,128]{1,2,0:T(8,128)S(1)}, f32[6,1,128]{1,2,0:T(8,128)S(1)}, u32[]{:S(2)}, u32[]{:S(2)}) collective-permute-start(f32[6,1,128]{1,2,0:T(8,128)S(1)} %get-tuple-element.505), channel_id=1, source_target_pairs={{0,1},{1,2},{2,3},{4,5},{5,6},{6,7},{8,9},{9,10},{10,11},{12,13},{... | collective-permute-start | bytes 9224 | tf_op jit(solution)/shard_map/ppermute | solution.py:14
  (7 other events, 48.4 us)
Sparse Core Ops, SparseCore 0:
  9.5 35.1 all-gather.1
